TPU v7x, 16 devices: a 4x2x1 block of a 4x4x8 slice. The times are simulated.
16 devices in a mesh: dp: 2 (over y, z), tp: 8 (over x, core).
Axes of the slice: x: 4, y: 2, z: 1, core: 2. Of those that a mesh axis runs over, the one named last changes fastest.
The devices are a block of a 4x4x8 slice.
Arguments:
- x_in: bfloat16 [2, 128, 5120], P('dp', 'tp'), parts along dimension 0
- start_pos: int32 [2], P('dp'), parts along dimension 0
- k_cache: bfloat16 [2, 4096, 8, 128], P('dp', None, 'tp'), parts along dimension 0
- v_cache: bfloat16 [2, 4096, 8, 128], P('dp', None, 'tp'), parts along dimension 0
- attn_gain: bfloat16 [5120], replicated
- w_query: bfloat16 [5120, 32, 128], P(None, 'tp')
- w_key: bfloat16 [5120, 8, 128], P(None, 'tp')
- w_value: bfloat16 [5120, 8, 128], P(None, 'tp')
- w_out: bfloat16 [32, 128, 5120], P('tp')
- mlp_gain: bfloat16 [5120], replicated
- w_gate: bfloat16 [5120, 14336], P(None, 'tp')
- w_up: bfloat16 [5120, 14336], P(None, 'tp')
- w_down: bfloat16 [14336, 5120], P('tp')
Outputs:
- output 1: bfloat16 [2, 128, 5120], P('dp', 'tp'), parts along dimension 0
- output 2: bfloat16 [2, 4096, 8, 128], P('dp', None, 'tp'), parts along dimension 0
- output 3: bfloat16 [2, 4096, 8, 128], P('dp', None, 'tp'), parts along dimension 0
There are 2 independent parts. A program takes and returns all parts, laid end to end along the dimension named above; an argument that names none is the same for every part.
All inputs are finite; a program needn't handle non-finite values.
Results may differ from a plain program's by a relative error of at most 0.0147496.
Values are sent between devices in bfloat16 or wider.
A program may use at most 768 MiB of HBM per device.

v0:
```python
import jax
import jax.numpy as jnp
from jax import lax
from jax.sharding import PartitionSpec as P

ROPE_BASE = 10000.0
NORM_EPS = 1e-5


def rms_norm(rows, gain):
    rows32 = rows.astype(jnp.float32)
    inv_rms = lax.rsqrt(jnp.mean(rows32 * rows32, axis=-1, keepdims=True) + NORM_EPS)
    return (rows32 * inv_rms * gain.astype(jnp.float32)).astype(jnp.bfloat16)


def rotate(heads_in, positions):
    head_dim = heads_in.shape[-1]
    inv_freq = jnp.power(ROPE_BASE, -jnp.arange(0, head_dim, 2).astype(jnp.float32) / head_dim)
    angles = positions.astype(jnp.float32)[..., None] * inv_freq
    lead = angles.shape[:2] + (1,) * (heads_in.ndim - 3) + (head_dim // 2,)
    cos_t = jnp.cos(angles).reshape(lead)
    sin_t = jnp.sin(angles).reshape(lead)
    pairs = heads_in.reshape(heads_in.shape[:-1] + (head_dim // 2, 2))
    even = pairs[..., 0]
    odd = pairs[..., 1]
    turned = jnp.stack([even * cos_t - odd * sin_t, even * sin_t + odd * cos_t], axis=-1)
    return turned.reshape(heads_in.shape)


def project_qkv(normed, positions, w_query, w_key, w_value):
    model_dim, kv_loc, head_dim = w_key.shape
    group = w_query.shape[1] // kv_loc
    w_query4 = w_query.reshape(model_dim, kv_loc, group, head_dim)
    q_lin = jnp.einsum('btd,dkge->btkge', normed, w_query4, preferred_element_type=jnp.float32)
    k_lin = jnp.einsum('btd,dke->btke', normed, w_key, preferred_element_type=jnp.float32)
    v_chunk = jnp.einsum('btd,dke->btke', normed, w_value, preferred_element_type=jnp.float32).astype(jnp.bfloat16)
    queries = rotate(q_lin, positions).astype(jnp.bfloat16)
    k_chunk = rotate(k_lin, positions).astype(jnp.bfloat16)
    return queries, k_chunk, v_chunk


def attend(queries, k_chunk, v_chunk, k_cache, v_cache, start_pos, tile_rows):
    rows, chunk_len, kv_loc, group, head_dim = queries.shape
    window = k_cache.shape[1]
    q_block = chunk_len
    while q_block > 8 and tile_rows * q_block > 256:
        q_block = q_block // 2
    n_blocks = chunk_len // q_block
    scale = head_dim ** -0.5
    offsets = jnp.mod(jnp.arange(window)[None, :] - start_pos[:, None], window)
    cache_valid = (start_pos[:, None] - window + offsets) >= 0
    key_ids = jnp.arange(chunk_len)

    def one_block(block):
        first = block * q_block
        q_tile = lax.dynamic_slice_in_dim(queries, first, q_block, axis=1)
        q_ids = first + jnp.arange(q_block)
        cache_mask = cache_valid[:, None, :] & (offsets[:, None, :] > q_ids[None, :, None])
        chunk_mask = key_ids[None, :] <= q_ids[:, None]
        s_cache = jnp.einsum('bqkge,bske->bkgqs', q_tile, k_cache, preferred_element_type=jnp.float32) * scale
        s_chunk = jnp.einsum('bqkge,bske->bkgqs', q_tile, k_chunk, preferred_element_type=jnp.float32) * scale
        s_cache = jnp.where(cache_mask[:, None, None], s_cache, -jnp.inf)
        s_chunk = jnp.where(chunk_mask, s_chunk, -jnp.inf)
        top = jnp.maximum(jnp.max(s_cache, axis=-1, keepdims=True), jnp.max(s_chunk, axis=-1, keepdims=True))
        e_cache = jnp.exp(s_cache - top)
        e_chunk = jnp.exp(s_chunk - top)
        total_mass = jnp.sum(e_cache, axis=-1, keepdims=True) + jnp.sum(e_chunk, axis=-1, keepdims=True)
        p_cache = (e_cache / total_mass).astype(jnp.bfloat16)
        p_chunk = (e_chunk / total_mass).astype(jnp.bfloat16)
        mixed = jnp.einsum('bkgqs,bske->bqkge', p_cache, v_cache, preferred_element_type=jnp.float32)
        mixed = mixed + jnp.einsum('bkgqs,bske->bqkge', p_chunk, v_chunk, preferred_element_type=jnp.float32)
        return mixed.astype(jnp.bfloat16)

    tiles = lax.map(one_block, jnp.arange(n_blocks))
    return tiles.reshape(n_blocks, rows, q_block, kv_loc * group, head_dim)


def write_chunk(cache, chunk, start_pos):
    window = cache.shape[1]
    chunk_len = chunk.shape[1]

    def one_row(old_rows, new_rows, start):
        filler = jnp.zeros((window - chunk_len,) + new_rows.shape[1:], new_rows.dtype)
        doubled = jnp.concatenate([new_rows, filler, new_rows, filler], axis=0)
        shift = jnp.mod(start, window)
        placed = lax.dynamic_slice_in_dim(doubled, window - shift, window, axis=0)
        offsets = jnp.mod(jnp.arange(window) - start, window)
        return jnp.where((offsets < chunk_len)[:, None, None], placed, old_rows)

    return jax.vmap(one_row)(cache, chunk, start_pos)


def swiglu(mlp_rows, w_gate, w_up):
    gate = jnp.einsum('btd,df->btf', mlp_rows, w_gate, preferred_element_type=jnp.float32)
    up_proj = jnp.einsum('btd,df->btf', mlp_rows, w_up, preferred_element_type=jnp.float32)
    return (jax.nn.silu(gate) * up_proj).astype(jnp.bfloat16)


def solution(mesh):
    row_spec = P('dp', 'tp', None)
    cache_spec = P('dp', None, 'tp', None)
    head_cols = P(None, 'tp', None)
    in_specs = (row_spec, P('dp'), cache_spec, cache_spec, P(), head_cols, head_cols, head_cols, P('tp', None, None), P(), P(None, 'tp'), P(None, 'tp'), P('tp', None))
    out_specs = (row_spec, cache_spec, cache_spec)

    def local_layer(x_in, start_pos, k_cache, v_cache, attn_gain, w_query, w_key, w_value, w_out, mlp_gain, w_gate, w_up, w_down):
        rows = x_in.shape[0]
        model_dim = x_in.shape[2]
        attn_rows = lax.all_gather(rms_norm(x_in, attn_gain), 'tp', axis=1, tiled=True)
        chunk_len = attn_rows.shape[1]
        positions = start_pos[:, None] + jnp.arange(chunk_len)[None, :]
        queries, k_chunk, v_chunk = project_qkv(attn_rows, positions, w_query, w_key, w_value)
        mixed = attend(queries, k_chunk, v_chunk, k_cache, v_cache, start_pos, rows)
        attn_part = jnp.einsum('nbqhe,hed->bnqd', mixed, w_out, preferred_element_type=jnp.float32)
        attn_part = attn_part.reshape(rows, chunk_len, model_dim).astype(jnp.bfloat16)
        attn_sum = lax.psum_scatter(attn_part, 'tp', scatter_dimension=1, tiled=True)
        hidden = (x_in.astype(jnp.float32) + attn_sum.astype(jnp.float32)).astype(jnp.bfloat16)
        mlp_rows = lax.all_gather(rms_norm(hidden, mlp_gain), 'tp', axis=1, tiled=True)
        activated = swiglu(mlp_rows, w_gate, w_up)
        mlp_part = jnp.einsum('btf,fd->btd', activated, w_down, preferred_element_type=jnp.float32).astype(jnp.bfloat16)
        mlp_sum = lax.psum_scatter(mlp_part, 'tp', scatter_dimension=1, tiled=True)
        x_out = (hidden.astype(jnp.float32) + mlp_sum.astype(jnp.float32)).astype(jnp.bfloat16)
        return x_out, write_chunk(k_cache, k_chunk, start_pos), write_chunk(v_cache, v_chunk, start_pos)

    return jax.shard_map(local_layer, mesh=mesh, in_specs=in_specs, out_specs=out_specs, check_vma=False)
```

profile of v0, /device:TPU:112, one launch (start us, length us, event | category | flops | bytes accessed | tf_op | source)
XLA Modules:
  0.0 163.8 jit_solution(64204827419978766)
XLA Ops:
  7.2 0.0 copy-start
  7.2 0.1 all-gather.3.cloned.1.call-start
  7.3 0.8 convert_element_type.149
  8.1 1.1 fusion.53
  9.1 1.7 %fusion.55 = bf16[1,16,5120]{2,1,0:T(8,128)(2,1)} fusion(bf16[1,16,5120]{2,1,0:T(8,128)(2,1)} %param.13, f32[5120]{0:T(1024)S(1)} %convert_element_type.149, f32[16]{0:T(128)S(1)} %add_rsqrt_fusion.1), kind=kLoop, calls=%fused_computation.62 | loop fusion | flops 327680 | bytes 348224 | tf_op jit(solution)/shard_map/convert_element_type | solution.py:13
  10.8 0.1 all-gather.3.cloned.1.call-update
  10.9 0.1 reduce-scatter.3.cloned.1.call-start
  11.6 11.7 %copy.27 = bf16[4,128,5120]{2,0,1:T(4,128)(2,1)} copy(bf16[4,128,5120]{1,0,2:T(4,128)(2,1)} %bitcast.180) | data formatting | bytes 10485760 | tf_op jit(solution)/shard_map/btd,dkge->btkge/dot_general | solution.py:34
  23.3 1.6 copy.36
  24.9 1.4 reshape.606
  26.3 0.2 multiply_cosine_fusion.1
  26.5 0.4 fusion.9
  26.9 6.6 %all-gather.3.cloned.1.call-done = bf16[1,128,5120]{2,1,0:T(8,128)(2,1)} async-done(((bf16[1,16,5120]{2,1,0:T(8,128)(2,1)}), bf16[1,128,5120]{2,1,0:T(8,128)(2,1)}) %all-gather.3.cloned.1.call-update) | async-done | bytes 1310736 | tf_op jit(solution)/shard_map/all_gather | solution.py:109
  33.5 8.7 %fusion.27 = f32[1,128,1,4,64,2]{1,4,5,3,2,0:T(8,128)S(1)} fusion(bf16[4,64,2,5120]{3,0,2,1:T(4,128)(2,1)} %bitcast.181, bf16[1,128,5120]{2,1,0:T(8,128)(2,1)} %all-gather.3.cloned.1.call-done), kind=kOutput, calls=%fused_computation.40 | convolution fusion | flops 671088640 | bytes 6815744 | tf_op jit(solution)/shard_map/btd,dkge->btkge/dot_general | solution.py:34
  42.2 0.0 copy-start.2
  42.3 0.5 fusion.37
  42.8 0.2 fusion.78
  43.1 0.1 copy.34
  43.2 0.2 copy-done.2
  43.5 1.8 %fusion.92 = (f32[4,128]{1,0:T(4,128)S(1)}, f32[1,1,4,128,4096]{4,3,2,1,0:T(8,128)S(1)}) fusion(bf16[128,4,128]{0,2,1:T(8,128)(2,1)S(1)} %bitcast.183, bf16[1,4096,1,128]{3,1,2,0:T(8,128)(2,1)S(1)} %copy-done.2, pred[128,4096]{1,0:T(8,128)(4,1)S(1)} %fusion.9), kind=kOutput, calls=%fused_computation.117 | convolution fusion | flops 543161856 | bytes 10094592 | tf_op jit(solution)/shard_map/while/body/eval_jaxpr/bqkge,bske->bkgqs/dot_general | solution.py:60
  45.3 0.2 fusion.93
  45.5 0.1 fusion.61
  45.6 0.0 copy-start.8
  45.6 1.3 fusion
  46.9 2.3 %fusion.24 = f32[128,4,128]{0,2,1:T(8,128)S(1)} fusion(f32[4,128]{1,0:T(4,128)S(1)} %add.154, f32[1,1,4,128,4096]{4,3,2,1,0:T(8,128)S(1)} %get-tuple-element.62, f32[4,128]{1,0:T(4,128)S(1)} %max.9, bf16[1,4096,1,128]{3,1,2,0:T(8,128)(2,1)S(1)} %copy-done.8), kind=kOutput, calls=%fused_computation.39 | convolution fusion | flops 543162368 | bytes 9703424 | tf_op jit(solution)/shard_map/while/body/eval_jaxpr/bkgqs,bske->bqkge/dot_general | solution.py:70
  49.2 0.5 fusion.42
  49.7 0.0 copy-start.9
  49.7 0.0 copy-start.3
  49.7 4.7 %fusion.3 = bf16[1,128,5120]{2,1,0:T(8,128)(2,1)} fusion(bf16[4,128,5120]{2,1,0:T(8,128)(2,1)} %param.21, f32[128,4,128]{0,2,1:T(8,128)S(1)} %fusion.24, f32[1,1,4,128,128]{3,4,2,1,0:T(8,128)S(1)} %get-tuple-element.64, f32[4,128]{1,0:T(4,128)S(1)} %add.154, f32[4,128]{1,0:T(4,128)S(1)} %max.9, bf16[128,128]{1,0:T(8,128)(2,1)S(1)} %fusion.42), kind=kOutput, calls=%fused_computation.8 | convolution fusion | flops 688848896 | bytes 7114752 | tf_op jit(solution)/shard_map/nbqhe,hed->bnqd/dot_general | solution.py:114
  54.4 0.1 reduce-scatter.3.cloned.1.call-update
  54.4 0.1 all-gather.5.cloned.1.call-start
  54.5 28.7 %reduce-scatter.3.cloned.1.call-done = bf16[1,16,5120]{2,1,0:T(8,128)(2,1)} async-done(((bf16[1,128,5120]{2,1,0:T(8,128)(2,1)}), bf16[1,16,5120]{2,1,0:T(8,128)(2,1)}) %reduce-scatter.3.cloned.1.call-update) | async-done | bytes 163856 | tf_op jit(solution)/shard_map/reduce_scatter | solution.py:116
  83.2 1.1 fusion.57
  84.3 1.7 %fusion.59 = bf16[1,16,5120]{2,1,0:T(8,128)(2,1)} fusion(f32[5120]{0:T(1024)S(1)} %convert_element_type.168, f32[16]{0:T(128)S(1)} %add_rsqrt_fusion, bf16[1,16,5120]{2,1,0:T(8,128)(2,1)} %reduce-scatter.3.cloned.1.call-done, bf16[1,16,5120]{2,1,0:T(8,128)(2,1)S(1)} %copy-done.3), kind=kLoop, calls=%fused_computation.66 | loop fusion | flops 655360 | bytes 512064 | tf_op jit(solution)/shard_map/convert_element_type | solution.py:13
  86.0 0.1 all-gather.5.cloned.1.call-update
  86.0 0.1 reduce-scatter.5.cloned.1.call-start
  86.1 18.4 %all-gather.5.cloned.1.call-done = bf16[1,128,5120]{2,1,0:T(8,128)(2,1)} async-done(((bf16[1,16,5120]{2,1,0:T(8,128)(2,1)}), bf16[1,128,5120]{2,1,0:T(8,128)(2,1)}) %all-gather.5.cloned.1.call-update) | async-done | bytes 1310736 | tf_op jit(solution)/shard_map/all_gather | solution.py:118
  104.5 9.3 %fusion.12 = f32[128,1792]{1,0:T(8,128)S(1)} fusion(bf16[5120,1792]{1,0:T(8,128)(2,1)} %param.23, bf16[1,128,5120]{2,1,0:T(8,128)(2,1)} %all-gather.5.cloned.1.call-done), kind=kOutput, calls=%fused_computation.25 | convolution fusion | flops 2348810240 | bytes 20578304 | tf_op jit(solution)/shard_map/btd,df->btf/dot_general | solution.py:94
  113.8 0.0 slice-start.3
  113.8 9.3 %fusion.8 = bf16[128,1792]{1,0:T(8,128)(2,1)S(1)} fusion(bf16[5120,1792]{1,0:T(8,128)(2,1)} %param.24, bf16[1,128,5120]{2,1,0:T(8,128)(2,1)S(1)} %copy-done.4, f32[128,1792]{1,0:T(8,128)S(1)} %fusion.12), kind=kOutput, calls=%fused_computation.14 | convolution fusion | flops 2350186496 | bytes 21037056 | tf_op jit(solution)/shard_map/btd,df->btf/dot_general | solution.py:95
  123.1 3.6 %fusion.2 = bf16[1,128,5120]{2,1,0:T(8,128)(2,1)} fusion(bf16[128,1792]{1,0:T(8,128)(2,1)S(1)} %fusion.8, bf16[1792,5120]{1,0:T(8,128)(2,1)S(1)} %bitcast.179), kind=kOutput, calls=%fused_computation.7 | convolution fusion | flops 2349465600 | bytes 20119552 | tf_op jit(solution)/shard_map/btf,fd->btd/dot_general | solution.py:120
  126.8 0.1 reduce-scatter.5.cloned.1.call-update
  126.9 0.1 copy.43
  127.1 0.0 copy-start.1
  127.1 0.1 broadcast.426
  127.2 8.6 %fusion.48 = (bf16[1,4096,1,128]{3,1,2,0:T(8,128)(2,1)}, bf16[1,4096,1,128]{3,1,2,0:T(8,128)(2,1)}) fusion(bf16[1,4096,1,128]{3,1,2,0:T(8,128)(2,1)} %param.16, s32[]{:T(128)} %bitcast.49, bf16[1,3968,1,128]{3,1,2,0:T(8,128)(2,1)S(1)} %broadcast.426, bf16[1,128,1,128]{3,1,2,0:T(8,128)(2,1)S(1)} %bitcast.184, pred[4096]{0:T(1024)(128)(4,1)S(1)} %broadcast_compare_fusion, ...), kind=kLoop, calls=%fused_computation.49 | loop fusion | flops 9437184 | bytes 5279748 | tf_op jit(solution)/shard_map/vmap(jit(_where))/select_n | solution.py:88
  135.9 19.7 %reduce-scatter.5.cloned.1.call-done = bf16[1,16,5120]{2,1,0:T(8,128)(2,1)} async-done(((bf16[1,128,5120]{2,1,0:T(8,128)(2,1)}), bf16[1,16,5120]{2,1,0:T(8,128)(2,1)}) %reduce-scatter.5.cloned.1.call-update) | async-done | bytes 163856 | tf_op jit(solution)/shard_map/reduce_scatter | solution.py:121
  155.6 1.6 %fusion.60 = bf16[1,16,5120]{2,1,0:T(8,128)(2,1)} fusion(bf16[1,16,5120]{2,1,0:T(8,128)(2,1)} %reduce-scatter.5.cloned.1.call-done, bf16[1,16,5120]{2,1,0:T(8,128)(2,1)S(1)} %copy-done.5, bf16[1,16,5120]{2,1,0:T(8,128)(2,1)S(1)} %copy-done.3), kind=kLoop, calls=%fused_computation.67 | loop fusion | flops 655360 | bytes 655360 | tf_op jit(solution)/shard_map/convert_element_type | solution.py:122
  (41 shorter events, 0.3 us)
Async XLA Ops:
  7.2 42.0 %copy-start = (bf16[5120,1,128]{2,0,1:T(8,128)(2,1)S(1)}, bf16[5120,1,128]{2,0,1:T(8,128)(2,1)}, u32[]{:S(2)}) copy-start(bf16[5120,1,128]{2,0,1:T(8,128)(2,1)} %param.20) | copy-start | bytes 3932164
  7.2 26.3 %all-gather.3.cloned.1.call-start = ((), (), s32[]{:S(2)}) async-start(), calls=%async_computation.2 | async-start | bytes 1474560 | tf_op jit(solution)/shard_map/all_gather | solution.py:109
  10.9 72.3 %reduce-scatter.3.cloned.1.call-start = ((), (), s32[]{:S(2)}) async-start(), calls=%async_computation.3 | async-start | bytes 1474560 | tf_op jit(solution)/shard_map/reduce_scatter | solution.py:116
  33.4 8.9 %copy-start.6 = (bf16[64,2,5120]{2,1,0:T(2,128)(2,1)S(1)}, bf16[64,2,5120]{2,1,0:T(2,128)(2,1)}, u32[]{:S(2)}) copy-start(bf16[64,2,5120]{2,1,0:T(2,128)(2,1)} %reshape.606) | copy-start | bytes 3932164
  33.4 8.9 %copy-start.7 = (bf16[1,128,5120]{2,1,0:T(8,128)(2,1)S(1)}, bf16[1,128,5120]{2,1,0:T(8,128)(2,1)}, u32[]{:S(2)}) copy-start(bf16[1,128,5120]{2,1,0:T(8,128)(2,1)} %all-gather.3.cloned.1.call-done) | copy-start | bytes 3932164
  42.2 1.2 copy-start.2
  45.6 1.3 copy-start.8
  49.7 4.8 %copy-start.9 = (bf16[5120]{0:T(1024)(128)(2,1)S(1)}, bf16[5120]{0:T(1024)(128)(2,1)}, u32[]{:S(2)}) copy-start(bf16[5120]{0:T(1024)(128)(2,1)} %param.22) | copy-start | bytes 30724
  49.7 33.5 %copy-start.3 = (bf16[1,16,5120]{2,1,0:T(8,128)(2,1)S(1)}, bf16[1,16,5120]{2,1,0:T(8,128)(2,1)}, u32[]{:S(2)}) copy-start(bf16[1,16,5120]{2,1,0:T(8,128)(2,1)} %param.13) | copy-start | bytes 491524
  54.4 50.1 %all-gather.5.cloned.1.call-start = ((), (), s32[]{:S(2)}) async-start(), calls=%async_computation.4 | async-start | bytes 1474560 | tf_op jit(solution)/shard_map/all_gather | solution.py:118
  86.0 69.6 %reduce-scatter.5.cloned.1.call-start = ((), (), s32[]{:S(2)}) async-start(), calls=%async_computation.5 | async-start | bytes 1474560 | tf_op jit(solution)/shard_map/reduce_scatter | solution.py:121
  104.5 9.3 %copy-start.4 = (bf16[1,128,5120]{2,1,0:T(8,128)(2,1)S(1)}, bf16[1,128,5120]{2,1,0:T(8,128)(2,1)}, u32[]{:S(2)}) copy-start(bf16[1,128,5120]{2,1,0:T(8,128)(2,1)} %all-gather.5.cloned.1.call-done) | copy-start | bytes 3932164
  104.5 18.6 %slice-start = ((s8[18350080]{0:T(1024)(128)(4,1)}), s8[4194304]{0:T(1024)(128)(4,1)S(1)}, s32[]{:S(2)}) async-start(s8[18350080]{0:T(1024)(128)(4,1)} %bitcast.178), calls=%async_computation.6 | async-start | bytes 8388608
  104.5 18.6 %slice-start.1 = ((s8[18350080]{0:T(1024)(128)(4,1)}), s8[4194304]{0:T(1024)(128)(4,1)S(1)}, s32[]{:S(2)}) async-start(s8[18350080]{0:T(1024)(128)(4,1)} %bitcast.178), calls=%async_computation.7 | async-start | bytes 8388608
  104.5 18.6 %slice-start.2 = ((s8[18350080]{0:T(1024)(128)(4,1)}), s8[4194304]{0:T(1024)(128)(4,1)S(1)}, s32[]{:S(2)}) async-start(s8[18350080]{0:T(1024)(128)(4,1)} %bitcast.178), calls=%async_computation.8 | async-start | bytes 8388608
  113.8 9.3 %slice-start.3 = ((s8[18350080]{0:T(1024)(128)(4,1)}), s8[4194304]{0:T(1024)(128)(4,1)S(1)}, s32[]{:S(2)}) async-start(s8[18350080]{0:T(1024)(128)(4,1)} %bitcast.178), calls=%async_computation.9 | async-start | bytes 8388608
  113.8 9.3 %slice-start.4 = ((s8[18350080]{0:T(1024)(128)(4,1)}), s8[1572864]{0:T(1024)(128)(4,1)S(1)}, s32[]{:S(2)}) async-start(s8[18350080]{0:T(1024)(128)(4,1)} %bitcast.178), calls=%async_computation.10 | async-start | bytes 3145728
  127.1 30.2 %copy-start.1 = (bf16[5120,1,128]{2,0,1:T(8,128)(2,1)S(1)}, bf16[5120,1,128]{2,0,1:T(8,128)(2,1)}, u32[]{:S(2)}) copy-start(bf16[5120,1,128]{2,0,1:T(8,128)(2,1)} %param.20) | copy-start | bytes 3932164
  127.2 28.4 %copy-start.5 = (bf16[1,16,5120]{2,1,0:T(8,128)(2,1)S(1)}, bf16[1,16,5120]{2,1,0:T(8,128)(2,1)}, u32[]{:S(2)}) copy-start(bf16[1,16,5120]{2,1,0:T(8,128)(2,1)} %reduce-scatter.3.cloned.1.call-done) | copy-start | bytes 491524
Sparse Core Ops, SparseCore 0:
  11.0 22.3 all-gather.2
  54.5 28.5 reduce-scatter.2
  86.1 18.2 all-gather.4
  127.0 28.5 reduce-scatter.4
where the time goes:
time: 164 us
  waiting for transfers between devices  73.5 us (45%)
  matrix products  40.9 us (25%)
  other arithmetic  18.9 us (12%)
  local copies, waits for them, and re-layouts  15.4 us (9%)
  between operations  14.8 us (9%)
    reduce_scatter x1, waiting for transfers between devices, local_layer(): lax.psum_scatter(attn_part, 'tp', scatter_dimension=1, tiled=True)  28.7 us
    reduce_scatter x1, waiting for transfers between devices, local_layer(): mlp_sum = lax.psum_scatter(mlp_part, 'tp', scatter_dimension=1, tiled=True)  19.7 us
    all_gather x1, waiting for transfers between devices, local_layer(): lax.all_gather(rms_norm(hidden, mlp_gain), 'tp', axis=1, tiled=True)  18.4 us
    dot_general x1, local copies, waits for them, and re-layouts, project_qkv(): jnp.einsum('btd,dkge->btkge', normed, w_query4, preferred_element_type=jn...  11.7 us
    dot_general x1, matrix products, swiglu(): jnp.einsum('btd,df->btf', mlp_rows, w_gate, preferred_element_type=jnp.fl...  9.3 us
    dot_general x1, matrix products, swiglu(): jnp.einsum('btd,df->btf', mlp_rows, w_up, preferred_element_type=jnp.floa...  9.26 us
    dot_general x1, matrix products, project_qkv(): jnp.einsum('btd,dkge->btkge', normed, w_query4, preferred_element_type=jn...  8.7 us
    select_n x1, other arithmetic, one_row(): return jnp.where((offsets < chunk_len)[:, None, None], placed, old_rows)  8.64 us
  transfers between devices with their start and end apart: 4, of which 4 were waited for; matrix products, arithmetic and copies ran while one was open for 15% of the time, Pallas kernels for 0%

commit v1 on v0

v1 whole, which is shorter than its diff:
```python
import functools

import jax
import jax.numpy as jnp
from jax import lax
from jax.experimental import pallas as pl
from jax.experimental.pallas import tpu as pltpu
from jax.sharding import PartitionSpec as P

ROPE_BASE = 10000.0
NORM_EPS = 1e-5
MESH = pl.DeviceIdType.MESH
BF16 = jnp.bfloat16
F32 = jnp.float32
SLOT = 256

LA, LB, RA, RB, OA, OB, PMA, PMB, PLA, PLB, PRA, PRB, POA, POB = range(14)


def layer_kernel(
    n_dev, dims,
    start_ref, x_ref, kc_hbm, vc_hbm, ag_ref, wq_hbm, wk_hbm, wv_hbm, wo_hbm, mg_ref, wg_hbm, wu_hbm, wd_hbm, cos_ref, sin_ref,
    xout_ref, kch_ref, vch_ref,
    g1, g2, nbuf, mbuf, part1, part2, prec1, prec2, rel1, rel2, fin1, fin2, ssbuf, arena, wo, raw, rawf, kt, kc, vc,
    qbuf, sbuf, obuf, acc, ubuf,
    loc_sem, raw_sem, gu_sem, wd_sem,
    a1_send, a1_recv, a2_send, a2_recv, ss_send, ss_recv, d1_send, d1_recv, d2_send, d2_recv, r1_send, r1_recv, r2_send, r2_recv,
):
    D, T, TL, HD, F, W, G = dims
    n_chip = n_dev // 2
    dblk = D // n_dev
    dchip = D // n_chip
    me = lax.axis_index("tp")
    chip = lax.div(me, 2)
    core = lax.rem(me, 2)
    other = 1 - core
    right = lax.rem(chip + 1, n_chip)
    left = lax.rem(chip + n_chip - 1, n_chip)
    opp = lax.rem(chip + 2, n_chip)
    partner = 2 * chip + other
    right_dev = 2 * right + core
    left_dev = 2 * left + core
    own = me

    half_n = T // 2

    x_in = pltpu.make_async_copy(x_ref, g1.at[own], loc_sem.at[0])
    x_in.start()

    n_raw = raw_sem.shape[0]
    raw_rows = raw.shape[1]

    def raw_copy(i):
        return pltpu.make_async_copy(wq_hbm.at[pl.ds(i * raw_rows, raw_rows)], raw.at[i % 2], raw_sem.at[i])

    R_KV, R_Q = 0, D
    gu_n = 2 * F // SLOT
    gu_rows = gu_n * dchip

    def gu_base(s):
        return gu_rows * (s + 1) if s < n_chip - 1 else 0

    order = (chip, left, right, opp)

    def gu_copy(s, n):
        src = wg_hbm if n < gu_n // 2 else wu_hbm
        nn = n % (gu_n // 2)
        rows = pl.ds(pl.multiple_of(order[s] * dchip, dchip), dchip)
        return pltpu.make_async_copy(src.at[rows, pl.ds(nn * SLOT, SLOT)], arena.at[pl.ds(gu_base(s) + n * dchip, dchip)], gu_sem.at[s, n])

    wd_base = gu_rows

    def wd_copy(j):
        return pltpu.make_async_copy(wd_hbm.at[:, pl.ds(j * SLOT, SLOT)], arena.at[pl.ds(wd_base + j * F, F)], wd_sem.at[j])

    wk_copy = pltpu.make_async_copy(wk_hbm, arena.at[pl.ds(R_KV, D), pl.ds(0, HD)], loc_sem.at[1])
    wv_copy = pltpu.make_async_copy(wv_hbm, arena.at[pl.ds(R_KV, D), pl.ds(HD, HD)], loc_sem.at[2])
    kc_copy = pltpu.make_async_copy(kc_hbm, kc, loc_sem.at[3])
    vc_copy = pltpu.make_async_copy(vc_hbm, vc, loc_sem.at[4])
    wo_copy = pltpu.make_async_copy(wo_hbm, wo, loc_sem.at[5])

    raw_copy(0).start()
    raw_copy(1).start()

    barrier = pltpu.get_barrier_semaphore()
    for k in range(1, n_dev):
        pl.semaphore_signal(barrier, inc=1, device_id={"tp": lax.rem(me + k, n_dev)}, device_id_type=MESH)
    pl.semaphore_wait(barrier, n_dev - 1)

    def gather(buf, send, recv):
        rows = buf.shape[1] // 2

        def copy(block, half, sem, dev):
            view = buf.at[block, pl.ds(half * rows, rows)]
            return pltpu.make_async_remote_copy(view, view, send.at[sem], recv.at[sem], device_id={"tp": dev}, device_id_type=MESH)

        own_a = [copy(own, 0, LA, right_dev), copy(own, 0, RA, left_dev), copy(own, 0, PMA, partner)]
        own_b = [copy(own, 1, RB, left_dev), copy(own, 1, LB, right_dev), copy(own, 1, PMB, partner)]
        relay_a = copy(2 * left + core, 0, OA, right_dev)
        relay_b = copy(2 * right + core, 1, OB, left_dev)
        fwd = {
            LA: copy(2 * left + core, 0, PLA, partner), LB: copy(2 * left + core, 1, PLB, partner),
            RA: copy(2 * right + core, 0, PRA, partner), RB: copy(2 * right + core, 1, PRB, partner),
            OA: copy(2 * opp + core, 0, POA, partner), OB: copy(2 * opp + core, 1, POB, partner),
        }
        arrive = {
            LA: copy(2 * left + core, 0, LA, partner), LB: copy(2 * left + core, 1, LB, partner),
            RA: copy(2 * right + core, 0, RA, partner), RB: copy(2 * right + core, 1, RB, partner),
            OA: copy(2 * opp + core, 0, OA, partner), OB: copy(2 * opp + core, 1, OB, partner),
            PMA: copy(2 * chip + other, 0, PMA, partner), PMB: copy(2 * chip + other, 1, PMB, partner),
            PLA: copy(2 * left + other, 0, PLA, partner), PLB: copy(2 * left + other, 1, PLB, partner),
            PRA: copy(2 * right + other, 0, PRA, partner), PRB: copy(2 * right + other, 1, PRB, partner),
            POA: copy(2 * opp + other, 0, POA, partner), POB: copy(2 * opp + other, 1, POB, partner),
        }

        def on_arrival(sem):
            arrive[sem].wait_recv()
            if sem == LA:
                relay_a.start()
            if sem == RB:
                relay_b.start()
            if sem in fwd:
                fwd[sem].start()

        def drain():
            for c in own_a + own_b + [relay_a, relay_b] + list(fwd.values()):
                c.wait_send()

        return own_a, own_b, on_arrival, drain

    a1_a, a1_b, a1_arrive, a1_drain = gather(g1, a1_send, a1_recv)
    x_in.wait()
    for c in a1_a + a1_b:
        c.start()

    wk_copy.start()
    wv_copy.start()
    kc_copy.start()

    rf_rows = rawf.shape[0]

    def split_heads(i):
        raw_copy(i).wait()

        def body(j, carry):
            rawf[...] = raw[i % 2, pl.ds(pl.multiple_of(j * rf_rows, rf_rows), rf_rows), :].astype(F32)
            d0 = pl.multiple_of(i * (raw_rows // G) + j * (rf_rows // G), rf_rows // G)
            for h in range(G):
                piece = rawf[pl.ds(h, rf_rows // G, stride=G), :].astype(BF16)
                arena[pl.ds(R_Q + (h // 2) * D + d0, rf_rows // G), pl.ds((h % 2) * HD, HD)] = piece
            return carry

        lax.fori_loop(0, raw_rows // rf_rows, body, 0)
        if i + 2 < n_raw:
            raw_copy(i + 2).start()

    def norm_block(b):
        xb = g1[b].astype(F32)
        inv = lax.rsqrt(jnp.mean(xb * xb, axis=-1, keepdims=True) + NORM_EPS)
        nbuf[pl.ds(pl.multiple_of(b * TL, TL), TL), :] = (xb * inv * ag_ref[...].astype(F32)).astype(BF16)

    split_heads(0)
    vc_copy.start()
    wo_copy.start()
    split_heads(1)
    for s in range(n_chip - 1):
        for n in range(gu_n):
            gu_copy(s, n).start()
    a1_arrive(LA)
    a1_arrive(RB)
    split_heads(2)
    norm_block(own)
    a1_arrive(LB)
    a1_arrive(RA)
    split_heads(3)
    norm_block(2 * left + core)
    norm_block(2 * right + core)
    kc_copy.wait()

    def kt_body(i, carry):
        r0 = pl.multiple_of(i * HD, HD)
        kt[:, pl.ds(r0, HD)] = kc[pl.ds(r0, HD), :].astype(F32).T.astype(BF16)
        return carry

    lax.fori_loop(0, W // HD, kt_body, 0)
    a1_arrive(PMA)
    a1_arrive(PMB)
    norm_block(2 * chip + other)
    a1_arrive(PLA)
    a1_arrive(PLB)
    norm_block(2 * left + other)
    a1_arrive(PRA)
    a1_arrive(PRB)
    norm_block(2 * right + other)
    a1_arrive(OA)
    a1_arrive(OB)
    norm_block(2 * opp + core)
    a1_arrive(POA)
    a1_arrive(POB)
    norm_block(2 * opp + other)

    lane = lax.broadcasted_iota(jnp.int32, (T, HD), 1)
    is_even = lax.rem(lane, 2) == 0

    def turn(v):
        swapped = jnp.where(is_even, pltpu.roll(v, HD - 1, 1), pltpu.roll(v, 1, 1))
        return v * cos_ref[...] + swapped * sin_ref[...]

    wk_copy.wait()
    wv_copy.wait()
    kv = jnp.dot(nbuf[...], arena[pl.ds(R_KV, D), :], preferred_element_type=F32)
    kch_ref[...] = turn(kv[:, :HD]).astype(BF16)
    vch_ref[...] = kv[:, HD:].astype(BF16)
    for j in range(G // 2):
        q2 = jnp.dot(nbuf[...], arena[pl.ds(R_Q + j * D, D), :], preferred_element_type=F32)
        for hh in range(2):
            qh = turn(q2[:, hh * HD:(hh + 1) * HD]).astype(BF16)
            h = 2 * j + hh
            for u in range(2):
                qbuf[u, h * half_n:(h + 1) * half_n, :] = qh[u * half_n:(u + 1) * half_n]
    for n in range(gu_n):
        gu_copy(n_chip - 1, n).start()

    scale = HD ** -0.5
    start = start_ref[0]
    shift = lax.rem(start, W)
    rows_u = 2 * half_n
    cw = 256
    row_tok = lax.broadcasted_iota(jnp.int32, (rows_u, 1), 0)
    row_tok = jnp.where(row_tok >= half_n, row_tok - half_n, row_tok)

    def attend(u, j):
        q_u = qbuf[u, j * rows_u:(j + 1) * rows_u, :]
        q_id = row_tok + u * half_n
        s_c = lax.dot_general(q_u, kch_ref[...], (((1,), (1,)), ((), ())), preferred_element_type=F32) * scale
        s_c = jnp.where(lax.broadcasted_iota(jnp.int32, (rows_u, T), 1) <= q_id, s_c, -jnp.inf)
        top = jnp.max(s_c, axis=-1, keepdims=True)
        tops = jnp.full((rows_u, HD), -jnp.inf, F32)
        for c in range(W // cw):
            s = jnp.dot(q_u, kt[:, c * cw:(c + 1) * cw], preferred_element_type=F32) * scale
            off = c * cw + lax.broadcasted_iota(jnp.int32, (1, cw), 1) - shift
            off = jnp.where(off < 0, off + W, off)
            off = jnp.where(start - W + off >= 0, off, -1)
            s = jnp.where(off > q_id, s, -jnp.inf)
            sbuf[:, c * cw:(c + 1) * cw] = s
            for k in range(cw // HD):
                tops = jnp.maximum(tops, s[:, k * HD:(k + 1) * HD])
        top = jnp.maximum(top, jnp.max(tops, axis=-1, keepdims=True))
        e_c = jnp.exp(s_c - top)
        mass = e_c
        for c in range(W // cw):
            e = jnp.exp(sbuf[:, c * cw:(c + 1) * cw] - top)
            sbuf[:, c * cw:(c + 1) * cw] = e
            for k in range(cw // HD):
                mass = mass + e[:, k * HD:(k + 1) * HD]
        inv = 1.0 / jnp.sum(mass, axis=-1, keepdims=True)
        p_c = (e_c * inv).astype(BF16)
        p = (sbuf[...] * inv).astype(BF16)
        mixed = jnp.dot(p, vc[...], preferred_element_type=F32)
        mixed = mixed + jnp.dot(p_c, vch_ref[...], preferred_element_type=F32)
        mixed = mixed.astype(BF16)
        for hh in range(2):
            h = 2 * j + hh
            obuf[u, :, h * HD:(h + 1) * HD] = mixed[hh * half_n:(hh + 1) * half_n]

    chips = (opp, right, left, chip)

    def scatter(part, prec, rel, fin, u, d_send, d_recv, r_send, r_recv):
        rows = part.shape[3] // 2

        def view(ref, d, half):
            return ref.at[core, d, u, pl.ds(half * rows, rows)]

        def to_partner(o):
            return pltpu.make_async_remote_copy(
                part.at[other, chips[o], u], prec.at[chips[o], u], d_send.at[u, o], d_recv.at[u, o],
                device_id={"tp": partner}, device_id_type=MESH)

        def ring(src, dst, k, dev):
            return pltpu.make_async_remote_copy(src, dst, r_send.at[u, k], r_recv.at[u, k], device_id={"tp": dev}, device_id_type=MESH)

        opp_a = ring(view(part, opp, 0), rel.at[0, u], 0, right_dev)
        opp_b = ring(view(part, opp, 1), rel.at[1, u], 1, left_dev)
        right_a = ring(view(part, right, 0), fin.at[0, u], 2, right_dev)
        right_b = ring(view(part, right, 1), fin.at[1, u], 3, right_dev)
        left_a = ring(view(part, left, 0), fin.at[2, u], 4, left_dev)
        left_b = ring(view(part, left, 1), fin.at[3, u], 5, left_dev)

        def add_partner(o):
            to_partner(o).wait_recv()
            d = chips[o]
            mine = part[core, d, u].astype(F32) + prec[d, u].astype(F32)
            part[core, d, u] = mine.astype(BF16)

        def first():
            add_partner(0)
            opp_a.start()
            opp_b.start()
            add_partner(1)
            right_b.start()
            add_partner(2)
            left_a.start()

        def relay():
            opp_a.wait_recv()
            a = view(part, right, 0)
            a[...] = (a[...].astype(F32) + rel[0, u].astype(F32)).astype(BF16)
            right_a.start()
            opp_b.wait_recv()
            b = view(part, left, 1)
            b[...] = (b[...].astype(F32) + rel[1, u].astype(F32)).astype(BF16)
            left_b.start()

        def total():
            to_partner(3).wait_recv()
            for c in (right_a, right_b, left_a, left_b):
                c.wait_recv()
            mine = part[core, chip, u].astype(F32) + prec[chip, u].astype(F32)
            out = []
            for half in range(2):
                sl = slice(half * rows, (half + 1) * rows)
                out.append(mine[sl] + fin[half, u].astype(F32) + fin[2 + half, u].astype(F32))
            return out

        def drain():
            for o in range(4):
                to_partner(o).wait_send()
            for c in (opp_a, opp_b, right_a, right_b, left_a, left_b):
                c.wait_send()

        return to_partner, first, relay, total, drain

    rs1 = [scatter(part1, prec1, rel1, fin1, u, d1_send, d1_recv, r1_send, r1_recv) for u in range(2)]
    n_jj = dchip // SLOT

    def project_out(u):
        o_u = obuf[u]
        for o in range(4):
            d = chips[o]
            for jj in range(n_jj):
                cols = pl.ds(pl.multiple_of(d * dchip + jj * SLOT, SLOT), SLOT)
                res = jnp.dot(o_u, wo[:, cols], preferred_element_type=F32).astype(BF16)
                for k in range(SLOT // HD):
                    c0 = jj * SLOT + k * HD
                    part1[c0 // dblk, d, u, :, c0 % dblk:c0 % dblk + HD] = res[:, k * HD:(k + 1) * HD]
            rs1[u][0](o).start()

    my_cols = pl.ds(pl.multiple_of(me * dblk, 128), dblk)
    a2_a, a2_b, a2_arrive, a2_drain = gather(g2, a2_send, a2_recv)

    def hidden_rows(u):
        per = half_n // TL
        hb = []
        for half, sums in enumerate(rs1[u][3]()):
            xs = jnp.concatenate([g1[u * per + half * (per // 2) + i, :, my_cols] for i in range(per // 2)], axis=0)
            hid = (xs.astype(F32) + sums).astype(BF16)
            g2[own, u * half_n + half * (half_n // 2):u * half_n + (half + 1) * (half_n // 2), :] = hid
            h32 = hid.astype(F32)
            hb.append(jnp.sum(h32 * h32, axis=-1, keepdims=True))
        return hb

    vc_copy.wait()
    attend(0, 0)
    attend(0, 1)
    wo_copy.wait()
    project_out(0)
    attend(1, 0)
    rs1[0][1]()
    attend(1, 1)
    rs1[0][2]()
    project_out(1)
    rs1[1][1]()
    ss = hidden_rows(0)
    for c in a2_a:
        c.start()
    rs1[1][2]()
    ss = ss + hidden_rows(1)
    col = jnp.concatenate(ss, axis=0)
    row = jnp.broadcast_to(col, (T, T)).T[0:8]
    ssbuf[own] = row

    def ss_copy(src, k):
        dev = lax.rem(me + k, n_dev)
        return pltpu.make_async_remote_copy(ssbuf.at[src], ssbuf.at[src], ss_send.at[k - 1], ss_recv.at[k - 1], device_id={"tp": dev}, device_id_type=MESH)

    for c in a2_b:
        c.start()
    for k in range(1, n_dev):
        ss_copy(own, k).start()
    for k in range(1, n_dev):
        ss_copy(lax.rem(me + n_dev - k, n_dev), k).wait_recv()
    tot = ssbuf[0]
    for k in range(1, n_dev):
        tot = tot + ssbuf[k]
    inv_row = lax.rsqrt(tot[0:1] * (1.0 / D) + NORM_EPS)
    inv = jnp.broadcast_to(inv_row, (T, T)).T[:, 0:1]

    def gate_up(s):
        d = order[s]
        for c in range(2):
            b = 2 * d + c
            mbuf[:, c * dblk:(c + 1) * dblk] = (g2[b].astype(F32) * inv * mg_ref[b].astype(F32)).astype(BF16)
        for n in range(gu_n):
            gu_copy(s, n).wait()
            part = jnp.dot(mbuf[...], arena[gu_base(s) + n * dchip:gu_base(s) + (n + 1) * dchip, :], preferred_element_type=F32)
            if s:
                part = acc[:, n * SLOT:(n + 1) * SLOT] + part
            acc[:, n * SLOT:(n + 1) * SLOT] = part

    a2_arrive(PMA)
    a2_arrive(LA)
    a2_arrive(RB)
    a2_arrive(PMB)
    gate_up(0)
    wd_half = wd_sem.shape[0] // 2
    for j in range(wd_half):
        wd_copy(j).start()
    for s in (RA, LB, PLA, PLB):
        a2_arrive(s)
    gate_up(1)
    for j in range(wd_half, 2 * wd_half):
        wd_copy(j).start()
    a2_arrive(OA)
    a2_arrive(OB)
    a2_arrive(PRA)
    a2_arrive(PRB)
    gate_up(2)
    a2_arrive(POA)
    a2_arrive(POB)
    gate_up(3)
    half_g = gu_n // 2
    for n in range(half_g):
        gate = acc[:, n * SLOT:(n + 1) * SLOT]
        up = acc[:, (half_g + n) * SLOT:(half_g + n + 1) * SLOT]
        ubuf[:, n * SLOT:(n + 1) * SLOT] = (gate * (1.0 / (1.0 + jnp.exp(-gate))) * up).astype(BF16)

    n_q = n_chip
    rs2 = [scatter(part2, prec2, rel2, fin2, q, d2_send, d2_recv, r2_send, r2_recv) for q in range(n_q)]

    def down(q):
        for jj in range(n_jj):
            j = q * n_jj + jj
            wd_copy(j).wait()
            res = jnp.dot(ubuf[...], arena[wd_base + j * F:wd_base + (j + 1) * F, :], preferred_element_type=F32).astype(BF16)
            for b in range(n_dev):
                part2[b % 2, b // 2, q, :, jj * SLOT:(jj + 1) * SLOT] = res[b * TL:(b + 1) * TL]
        for o in range(4):
            rs2[q][0](o).start()

    def finish(q):
        sums = jnp.concatenate(rs2[q][3](), axis=0)
        tok = pl.ds(pl.multiple_of(me * TL, TL), TL)
        hid = jnp.concatenate([g2[2 * q + c, tok, :] for c in range(2)], axis=1)
        xout_ref[:, q * dchip:(q + 1) * dchip] = (hid.astype(F32) + sums).astype(BF16)

    down(0)
    down(1)
    rs2[0][1]()
    down(2)
    rs2[1][1]()
    down(3)
    rs2[2][1]()
    rs2[0][2]()
    rs2[3][1]()
    rs2[1][2]()
    rs2[2][2]()
    rs2[3][2]()
    for q in range(n_q):
        finish(q)

    a1_drain()
    a2_drain()
    for k in range(1, n_dev):
        ss_copy(own, k).wait_send()
    for r in rs1 + rs2:
        r[4]()


def write_chunk(cache, chunk, start_pos):
    window = cache.shape[1]
    chunk_len = chunk.shape[1]

    def one_row(old_rows, new_rows, start):
        filler = jnp.zeros((window - chunk_len,) + new_rows.shape[1:], new_rows.dtype)
        doubled = jnp.concatenate([new_rows, filler, new_rows, filler], axis=0)
        shift = jnp.mod(start, window)
        placed = lax.dynamic_slice_in_dim(doubled, window - shift, window, axis=0)
        offsets = jnp.mod(jnp.arange(window) - start, window)
        return jnp.where((offsets < chunk_len)[:, None, None], placed, old_rows)

    return jax.vmap(one_row)(cache, chunk, start_pos)


def solution(mesh):
    row_spec = P('dp', 'tp', None)
    cache_spec = P('dp', None, 'tp', None)
    head_cols = P(None, 'tp', None)
    in_specs = (row_spec, P('dp'), cache_spec, cache_spec, P(), head_cols, head_cols, head_cols, P('tp', None, None), P(), P(None, 'tp'), P(None, 'tp'), P('tp', None))
    out_specs = (row_spec, cache_spec, cache_spec)
    n_dev = mesh.shape['tp']

    def local_layer(x_in, start_pos, k_cache, v_cache, attn_gain, w_query, w_key, w_value, w_out, mlp_gain, w_gate, w_up, w_down):
        _, TL, D = x_in.shape
        W, HD = k_cache.shape[1], k_cache.shape[3]
        G = w_query.shape[1]
        F = w_gate.shape[1]
        T = TL * n_dev
        n_chip = n_dev // 2
        dblk, dchip = D // n_dev, D // n_chip
        inv_freq = jnp.power(ROPE_BASE, -jnp.arange(0, HD, 2).astype(F32) / HD)
        positions = start_pos[0] + jnp.arange(T)
        angles = positions.astype(F32)[:, None] * jnp.repeat(inv_freq, 2)[None, :]
        sign = jnp.where(jnp.arange(HD) % 2 == 0, -1.0, 1.0).astype(F32)
        cos_t = jnp.cos(angles)
        sin_t = jnp.sin(angles) * sign

        vmem = pl.BlockSpec(memory_space=pltpu.VMEM)
        hbm = pl.BlockSpec(memory_space=pl.ANY)
        smem = pl.BlockSpec(memory_space=pltpu.SMEM)
        gu_n = 2 * F // SLOT
        V = pltpu.VMEM
        dma = pltpu.SemaphoreType.DMA
        n_raw = 4
        raw_rows = D * G // n_raw
        half = T // 2
        scratch = [
            V((n_dev, TL, D), BF16), V((n_dev, T, dblk), BF16), V((T, D), BF16), V((T, dchip), BF16),
            V((2, n_chip, 2, half, dblk), BF16), V((2, n_chip, n_chip, TL, dchip), BF16),
            V((n_chip, 2, half, dblk), BF16), V((n_chip, n_chip, TL, dchip), BF16),
            V((2, 2, half // 2, dblk), BF16), V((2, n_chip, TL // 2, dchip), BF16),
            V((4, 2, half // 2, dblk), BF16), V((4, n_chip, TL // 2, dchip), BF16),
            V((n_dev, 8, T), F32),
            V((n_chip * gu_n * dchip, SLOT), BF16), V((G * HD, D), BF16),
            V((2, raw_rows, HD), BF16), V((512, HD), F32),
            V((HD, W), BF16), V((W, HD), BF16), V((W, HD), BF16),
            V((2, G * half, HD), BF16), V((2 * half, W), F32), V((2, half, G * HD), BF16),
            V((T, 2 * F), F32), V((T, F), BF16),
            dma((6,)), dma((n_raw,)), dma((n_chip, gu_n)), dma((D // SLOT,)),
            dma((14,)), dma((14,)), dma((14,)), dma((14,)), dma((n_dev - 1,)), dma((n_dev - 1,)),
            dma((2, 4)), dma((2, 4)), dma((n_chip, 4)), dma((n_chip, 4)),
            dma((2, 6)), dma((2, 6)), dma((n_chip, 6)), dma((n_chip, 6)),
        ]
        x_out, k_chunk, v_chunk = pl.pallas_call(
            functools.partial(layer_kernel, n_dev, (D, T, TL, HD, F, W, G)),
            out_shape=[jax.ShapeDtypeStruct((TL, D), BF16), jax.ShapeDtypeStruct((T, HD), BF16), jax.ShapeDtypeStruct((T, HD), BF16)],
            in_specs=[smem, hbm, hbm, hbm, vmem, hbm, hbm, hbm, hbm, vmem, hbm, hbm, hbm, vmem, vmem],
            out_specs=[vmem, vmem, vmem],
            scratch_shapes=scratch,
            compiler_params=pltpu.CompilerParams(collective_id=0, has_side_effects=True, vmem_limit_bytes=67043328),
            name="layer",
        )(
            start_pos, x_in[0], k_cache.reshape(W, HD), v_cache.reshape(W, HD), attn_gain.reshape(1, D),
            w_query.reshape(D * G, HD), w_key.reshape(D, HD), w_value.reshape(D, HD), w_out.reshape(G * HD, D),
            mlp_gain.reshape(n_dev, 1, dblk), w_gate, w_up, w_down, cos_t, sin_t,
        )
        k_chunk = k_chunk.reshape(1, T, 1, HD)
        v_chunk = v_chunk.reshape(1, T, 1, HD)
        return x_out[None], write_chunk(k_cache, k_chunk, start_pos), write_chunk(v_cache, v_chunk, start_pos)

    return jax.shard_map(local_layer, mesh=mesh, in_specs=in_specs, out_specs=out_specs, check_vma=False)
```

time: 164 us -> 97.9 us (0.60)
  Pallas kernels: 0 us -> 82.5 us
  waiting for transfers between devices: 73.5 us -> 0 us
  matrix products: 40.9 us -> 0 us
  between operations: 14.8 us -> 1.35 us
  local copies, waits for them, and re-layouts: 15.4 us -> 3.65 us
  other arithmetic: 18.9 us -> 10 us
    pallas_call x0 -> x1, Pallas kernels: none -> 82.5 us  [local_layer(): pl.pallas_call(functools.partial(layer_kernel, n_dev, (D, T, TL, HD, F, W...]
    reduce_scatter x2 -> x0, waiting for transfers between devices: 48.4 us -> none  [the longest x1 28.7 us: local_layer(): lax.psum_scatter(attn_part, 'tp', scatter_dimension=1, tiled=True)]
    dot_general x10 -> x0, matrix products: 40.9 us -> none  [the longest x1 9.3 us: swiglu(): jnp.einsum('btd,df->btf', mlp_rows, w_gate, preferred_element_type=jnp.fl...]
    all_gather x2 -> x0, waiting for transfers between devices: 24.9 us -> none  [the longest x1 18.4 us: local_layer(): lax.all_gather(rms_norm(hidden, mlp_gain), 'tp', axis=1, tiled=True)]
    dot_general x2 -> x0, local copies, waits for them, and re-layouts: 13.3 us -> none  [the longest x1 11.7 us: project_qkv(): jnp.einsum('btd,dkge->btkge', normed, w_query4, preferred_element_type=jn...]
    convert_element_type x6 -> x1, other arithmetic: 5.83 us -> 0.01 us  [local_layer(): angles = positions.astype(F32)[:, None] * jnp.repeat(inv_freq, 2)[None, :]]
    reduce_sum x4 -> x0, other arithmetic: 3.48 us -> none  [the longest x2 2.15 us: rms_norm(): jnp.mean(rows32 * rows32, axis=-1, keepdims=True) + NORM_EPS]
    reshape x0 -> x2, local copies, waits for them, and re-layouts: none -> 2.63 us  [the longest x1 1.32 us: local_layer(): attn_gain.reshape(1, D)]
  transfers between devices with their start and end apart: 4 -> 0, of which waited for: 4 -> 0; matrix products, arithmetic and copies ran while one was open for 15% -> 0% of each run, Pallas kernels for 0% -> 0%
where the time goes in v1:
time: 97.9 us; the launch traced here: 97.6 us
  Pallas kernels  82.5 us (84%)
  other arithmetic  10 us (10%)
  local copies, waits for them, and re-layouts  3.65 us (4%)
  between operations  1.35 us (1%)
    pallas_call x1, Pallas kernels, local_layer(): pl.pallas_call(functools.partial(layer_kernel, n_dev, (D, T, TL, HD, F, W...  82.5 us
    select_n x1, other arithmetic, one_row(): return jnp.where((offsets < chunk_len)[:, None, None], placed, old_rows)  8.43 us

profile of v1, /device:TPU:112, one launch (start us, length us, event | category | flops | bytes accessed | tf_op | source)
XLA Modules:
  0.0 97.6 jit_solution(18281387140678163291)
XLA Ops:
  1.3 0.6 fusion.10
  1.9 1.3 %reshape.87.ag_ref = bf16[1,5120]{1,0:T(2,128)(2,1)} reshape(bf16[5120]{0:T(1024)(128)(2,1)} %param.17) | data formatting | bytes 20480 | tf_op jit(solution)/shard_map/reshape | solution.py:552
  3.3 1.3 %reshape.152.mg_ref = bf16[8,1,640]{2,1,0:T(2,128)(2,1)} reshape(bf16[5120]{0:T(1024)(128)(2,1)} %param.22) | data formatting | bytes 20480 | tf_op jit(solution)/shard_map/reshape | solution.py:554
  4.6 0.1 broadcast_in_dim.37
  4.6 0.1 mul.32
  4.8 1.0 fusion.8
  5.8 82.5 %layer.1 = (bf16[16,5120]{1,0:T(8,128)(2,1)}, bf16[128,128]{1,0:T(8,128)(2,1)}, bf16[128,128]{1,0:T(8,128)(2,1)}) custom-call(s32[1]{0:T(128)} %copy.18.start_ref, bf16[16,5120]{1,0:T(8,128)(2,1)} %bitcast.20, bf16[4096,128]{1,0:T(8,128)(2,1)} %bitcast.16, bf16[4096,128]{1,0:T(8,128)(2,1)} %bitcast.17, bf16[1,5120]{1,0:T(2,128)(2,1)} %reshape.87.ag_ref, ...), custom_call_target="tpu_custom_call" | custom-call | tf_op jit(solution)/shard_map/layer/pallas_call | solution.py:543
  88.3 0.1 broadcast.99
  88.5 0.0 copy-start
  88.5 8.4 %fusion.5 = (bf16[1,4096,1,128]{3,1,2,0:T(8,128)(2,1)}, bf16[1,4096,1,128]{3,1,2,0:T(8,128)(2,1)}) fusion(bf16[1,4096,1,128]{3,1,2,0:T(8,128)(2,1)} %param.16, s32[]{:T(128)} %bitcast.10, bf16[1,3968,1,128]{3,1,2,0:T(8,128)(2,1)S(1)} %broadcast.99, bf16[1,128,1,128]{3,1,2,0:T(8,128)(2,1)} %bitcast.23, pred[4096]{0:T(1024)(128)(4,1)} %fusion.10, ...), kind=kLoop, calls=%fused_computation.11 | loop fusion | flops 9437184 | bytes 5279748 | tf_op jit(solution)/shard_map/vmap(jit(_where))/select_n | solution.py:489
  96.9 0.0 copy-done
  96.9 0.7 copy.19
  (3 shorter events, 0.0 us)
Async XLA Ops:
  88.5 8.4 %copy-start = (bf16[16,5120]{1,0:T(8,128)(2,1)S(1)}, bf16[16,5120]{1,0:T(8,128)(2,1)}, u32[]{:S(2)}) copy-start(bf16[16,5120]{1,0:T(8,128)(2,1)} %get-tuple-element.6) | copy-start | bytes 491524

commit v2 on v1

v2 whole, which is shorter than its diff:
```python
import functools

import jax
import jax.numpy as jnp
import numpy as np
from jax import lax
from jax.experimental import pallas as pl
from jax.experimental.pallas import tpu as pltpu
from jax.sharding import PartitionSpec as P

ROPE_BASE = 10000.0
NORM_EPS = 1e-5
MESH = pl.DeviceIdType.MESH
BF16 = jnp.bfloat16
F32 = jnp.float32
SLOT = 512
Q_COLS = 1024
scope = jax.named_scope

LA, LB, RA, RB, OA, OB, PMA, PMB, PLA, PLB, PRA, PRB, POA, POB = range(14)


def layer_kernel(
    n_dev, dims,
    start_ref, x_ref, kc_hbm, vc_hbm, ag_ref, wq_hbm, wk_hbm, wv_hbm, wo_hbm, mg_ref, wg_hbm, wu_hbm, wd_hbm, freq_ref,
    xout_ref, kn_hbm, vn_hbm,
    g1, g2, nbuf, mbuf, part1, part2, prec1, prec2, rel1, rel2, fin1, fin2, ssbuf, arena, wo, rawf, kt, kc, vc,
    qbuf, sbuf, obuf, acc, ubuf, kch_ref, vch_ref, again, mgain, cos_ref, sin_ref,
    loc_sem, raw_sem, kv_sem, gu_sem, wd_sem,
    a1_send, a1_recv, a2_send, a2_recv, ss_send, ss_recv, d1_send, d1_recv, d2_send, d2_recv, r1_send, r1_recv, r2_send, r2_recv,
):
    D, T, TL, HD, F, W, G = dims
    n_chip = n_dev // 2
    dblk = D // n_dev
    dchip = D // n_chip
    me = lax.axis_index("tp")
    chip = lax.div(me, 2)
    core = lax.rem(me, 2)
    other = 1 - core
    right = lax.rem(chip + 1, n_chip)
    left = lax.rem(chip + n_chip - 1, n_chip)
    opp = lax.rem(chip + 2, n_chip)
    partner = 2 * chip + other
    right_dev = 2 * right + core
    left_dev = 2 * left + core
    own = me

    half_n = T // 2

    x_in = pltpu.make_async_copy(x_ref, g1.at[own], loc_sem.at[0])
    x_in.start()

    gu_n = 2 * F // SLOT
    gu_rows = gu_n * dchip
    order = (chip, left, right, opp)

    def gu_base(s):
        return gu_rows * (s + 1) if s < n_chip - 1 else 0

    def gu_start(s):
        rows = pl.ds(pl.multiple_of(order[s] * dchip, dchip), dchip)
        for src, first in ((wg_hbm, 0), (wu_hbm, F)):
            c0 = 0
            while c0 < F:
                at = first + c0
                wide = min(SLOT - at % SLOT, F - c0)
                dst = arena.at[pl.ds(gu_base(s) + at // SLOT * dchip, dchip), pl.ds(at % SLOT, wide)]
                pltpu.make_async_copy(src.at[rows, pl.ds(c0, wide)], dst, gu_sem.at[s]).start(priority=1)
                c0 += wide

    def gu_wait(s):
        region = arena.at[pl.ds(gu_base(s), gu_rows)]
        pltpu.make_async_copy(region, region, gu_sem.at[s]).wait()

    wd_base = gu_rows
    wd_n = D // SLOT

    def wd_copy(j):
        return pltpu.make_async_copy(wd_hbm.at[:, pl.ds(j * SLOT, SLOT)], arena.at[pl.ds(wd_base + j * F, F)], wd_sem.at[j])

    n_raw = SLOT // HD
    raw_rows = D * G // n_raw
    raw_base = gu_base(n_chip - 2)

    def raw_view(i):
        return arena.at[pl.ds(raw_base, raw_rows), pl.ds(i * HD, HD)]

    def raw_copy(i):
        return pltpu.make_async_copy(wq_hbm.at[pl.ds(i * raw_rows, raw_rows)], raw_view(i), raw_sem.at[i])

    kv_rows = pl.ds(D, D // 2)
    kv_copies = [
        pltpu.make_async_copy(src.at[pl.ds(half * (D // 2), D // 2)], arena.at[kv_rows, pl.ds((2 * half + i) * HD, HD)], kv_sem.at[2 * half + i])
        for half in range(2) for i, src in enumerate((wk_hbm, wv_hbm))
    ]
    kc_copy = pltpu.make_async_copy(kc_hbm, kc, loc_sem.at[1])
    vc_copy = pltpu.make_async_copy(vc_hbm, vc, loc_sem.at[2])
    wo_copy = pltpu.make_async_copy(wo_hbm, wo, loc_sem.at[3])

    for i in range(n_raw):
        raw_copy(i).start()
    kc_copy.start()
    for c in kv_copies:
        c.start()
    vc_copy.start()
    wo_copy.start(priority=1)
    for s in range(n_chip - 2):
        gu_start(s)

    barrier = pltpu.get_barrier_semaphore()
    for k in range(1, n_dev):
        pl.semaphore_signal(barrier, inc=1, device_id={"tp": lax.rem(me + k, n_dev)}, device_id_type=MESH)
    pl.semaphore_wait(barrier, n_dev - 1)

    def gather(buf, send, recv):
        rows = buf.shape[1] // 2

        def copy(block, half, sem, dev):
            view = buf.at[block, pl.ds(half * rows, rows)]
            return pltpu.make_async_remote_copy(view, view, send.at[sem], recv.at[sem], device_id={"tp": dev}, device_id_type=MESH)

        own_a = [copy(own, 0, LA, right_dev), copy(own, 0, RA, left_dev), copy(own, 0, PMA, partner)]
        own_b = [copy(own, 1, RB, left_dev), copy(own, 1, LB, right_dev), copy(own, 1, PMB, partner)]
        relay_a = copy(2 * left + core, 0, OA, right_dev)
        relay_b = copy(2 * right + core, 1, OB, left_dev)
        fwd = {
            LA: copy(2 * left + core, 0, PLA, partner), LB: copy(2 * left + core, 1, PLB, partner),
            RA: copy(2 * right + core, 0, PRA, partner), RB: copy(2 * right + core, 1, PRB, partner),
            OA: copy(2 * opp + core, 0, POA, partner), OB: copy(2 * opp + core, 1, POB, partner),
        }
        arrive = {
            LA: copy(2 * left + core, 0, LA, partner), LB: copy(2 * left + core, 1, LB, partner),
            RA: copy(2 * right + core, 0, RA, partner), RB: copy(2 * right + core, 1, RB, partner),
            OA: copy(2 * opp + core, 0, OA, partner), OB: copy(2 * opp + core, 1, OB, partner),
            PMA: copy(2 * chip + other, 0, PMA, partner), PMB: copy(2 * chip + other, 1, PMB, partner),
            PLA: copy(2 * left + other, 0, PLA, partner), PLB: copy(2 * left + other, 1, PLB, partner),
            PRA: copy(2 * right + other, 0, PRA, partner), PRB: copy(2 * right + other, 1, PRB, partner),
            POA: copy(2 * opp + other, 0, POA, partner), POB: copy(2 * opp + other, 1, POB, partner),
        }

        def on_arrival(sem):
            arrive[sem].wait_recv()
            if sem == LA:
                relay_a.start()
            if sem == RB:
                relay_b.start()
            if sem in fwd:
                fwd[sem].start()

        def drain():
            for c in own_a + own_b + [relay_a, relay_b] + list(fwd.values()):
                c.wait_send()

        return own_a, own_b, on_arrival, drain

    a1_a, a1_b, a1_arrive, a1_drain = gather(g1, a1_send, a1_recv)
    x_in.wait()
    for c in (a1_a[0], a1_b[0], a1_b[1], a1_a[1], a1_a[2], a1_b[2]):
        c.start()


    rf_rows = rawf.shape[0]

    def split_heads(i):
        raw_copy(i).wait()

        def body(j, carry):
            rawf[...] = arena[pl.ds(raw_base + pl.multiple_of(j * rf_rows, rf_rows), rf_rows), i * HD:(i + 1) * HD].astype(F32)
            d0 = pl.multiple_of(i * (raw_rows // G) + j * (rf_rows // G), rf_rows // G)
            for h in range(G):
                arena[pl.ds(d0, rf_rows // G), h * HD:(h + 1) * HD] = rawf[pl.ds(h, rf_rows // G, stride=G), :].astype(BF16)
            return carry

        lax.fori_loop(0, raw_rows // rf_rows, body, 0)

    again[...] = ag_ref[...].astype(F32)
    mgain[...] = mg_ref[...].astype(F32)

    def norm_block(b):
        xb = g1[b].astype(F32)
        inv = lax.rsqrt(jnp.mean(xb * xb, axis=-1, keepdims=True) + NORM_EPS)
        gain = jnp.concatenate([again[i:i + 1, :] for i in range(D // HD)], axis=1)
        nbuf[pl.ds(pl.multiple_of(b * TL, TL), TL), :] = (xb * inv * gain).astype(BF16)

    kt_rows = 4 * HD

    def kt_body(i, carry):
        r0 = pl.multiple_of(i * kt_rows, kt_rows)
        kt[:, pl.ds(r0, kt_rows)] = kc[pl.ds(r0, kt_rows), :].astype(F32).T.astype(BF16)
        return carry

    lane = lax.broadcasted_iota(jnp.int32, (T, HD), 1)
    is_even = lax.rem(lane, 2) == 0

    with scope("split01"):
        split_heads(0)
        split_heads(1)
        norm_block(own)
    with scope("a1_first"):
        a1_arrive(LA)
        a1_arrive(RB)
    with scope("angles"):
        angles = (start_ref[0] + lax.broadcasted_iota(jnp.int32, (T, HD), 0)).astype(F32) * freq_ref[...]
        cos_ref[...] = jnp.cos(angles)
        sin_t = jnp.sin(angles)
        sin_ref[...] = jnp.where(is_even, -sin_t, sin_t)
    with scope("split23"):
        split_heads(2)
        split_heads(3)
        gu_start(n_chip - 2)
    with scope("a1_second"):
        a1_arrive(LB)
        a1_arrive(RA)
    with scope("norm3"):
        norm_block(2 * left + core)
        norm_block(2 * right + core)
    with scope("kt"):
        kc_copy.wait()
        lax.fori_loop(0, W // kt_rows, kt_body, 0)
    with scope("a1_near"):
        a1_arrive(PMA)
        a1_arrive(PMB)
        norm_block(2 * chip + other)
        a1_arrive(PLA)
        a1_arrive(PLB)
        norm_block(2 * left + other)
        a1_arrive(PRA)
        a1_arrive(PRB)
        norm_block(2 * right + other)
    with scope("a1_far"):
        a1_arrive(OA)
        a1_arrive(OB)
        norm_block(2 * opp + core)
        a1_arrive(POA)
        a1_arrive(POB)
        norm_block(2 * opp + other)

    def turn(v):
        swapped = jnp.where(is_even, pltpu.roll(v, HD - 1, 1), pltpu.roll(v, 1, 1))
        return v * cos_ref[...] + swapped * sin_ref[...]

    with scope("qkv"):
        for c in kv_copies:
            c.wait()
        kv = jnp.dot(nbuf[:, :D // 2], arena[kv_rows, 0:2 * HD], preferred_element_type=F32)
        kv = kv + jnp.dot(nbuf[:, D // 2:], arena[kv_rows, 2 * HD:4 * HD], preferred_element_type=F32)
        kch_ref[...] = turn(kv[:, :HD]).astype(BF16)
        vch_ref[...] = kv[:, HD:].astype(BF16)
        q_all = jnp.dot(nbuf[...], arena[pl.ds(0, D), :], preferred_element_type=F32)
        for h in range(G):
            qh = turn(q_all[:, h * HD:(h + 1) * HD]).astype(BF16)
            for u in range(2):
                qbuf[u, h * half_n:(h + 1) * half_n, :] = qh[u * half_n:(u + 1) * half_n]
        gu_start(n_chip - 1)

    scale = HD ** -0.5
    start = start_ref[0]
    shift = lax.rem(start, W)
    rows_u = 2 * half_n
    cw = 512
    row_tok = lax.broadcasted_iota(jnp.int32, (rows_u, 1), 0)
    row_tok = jnp.where(row_tok >= half_n, row_tok - half_n, row_tok)

    def attend(u, j):
        q_u = qbuf[u, j * rows_u:(j + 1) * rows_u, :]
        q_id = row_tok + u * half_n
        s_c = lax.dot_general(q_u, kch_ref[...], (((1,), (1,)), ((), ())), preferred_element_type=F32) * scale
        s_c = jnp.where(lax.broadcasted_iota(jnp.int32, (rows_u, T), 1) <= q_id, s_c, -jnp.inf)
        top = jnp.max(s_c, axis=-1, keepdims=True)
        tops = jnp.full((rows_u, HD), -jnp.inf, F32)
        for c in range(W // cw):
            s = jnp.dot(q_u, kt[:, c * cw:(c + 1) * cw], preferred_element_type=F32) * scale
            off = c * cw + lax.broadcasted_iota(jnp.int32, (1, cw), 1) - shift
            off = jnp.where(off < 0, off + W, off)
            off = jnp.where(start - W + off >= 0, off, -1)
            s = jnp.where(off > q_id, s, -jnp.inf)
            sbuf[:, c * cw:(c + 1) * cw] = s
            for k in range(cw // HD):
                tops = jnp.maximum(tops, s[:, k * HD:(k + 1) * HD])
        top = jnp.maximum(top, jnp.max(tops, axis=-1, keepdims=True))
        e_c = jnp.exp(s_c - top)
        mass = e_c
        for c in range(W // cw):
            e = jnp.exp(sbuf[:, c * cw:(c + 1) * cw] - top)
            sbuf[:, c * cw:(c + 1) * cw] = e
            for k in range(cw // HD):
                mass = mass + e[:, k * HD:(k + 1) * HD]
        inv = 1.0 / jnp.sum(mass, axis=-1, keepdims=True)
        p_c = (e_c * inv).astype(BF16)
        p = (sbuf[...] * inv).astype(BF16)
        mixed = jnp.dot(p, vc[...], preferred_element_type=F32)
        mixed = mixed + jnp.dot(p_c, vch_ref[...], preferred_element_type=F32)
        mixed = mixed.astype(BF16)
        for hh in range(2):
            h = 2 * j + hh
            obuf[u, :, h * HD:(h + 1) * HD] = mixed[hh * half_n:(hh + 1) * half_n]

    def new_cache(cache, chunk_ref, out_hbm, sem):
        token = lax.broadcasted_iota(jnp.int32, (T, T), 0) - lax.rem(start, T)
        token = jnp.where(token < 0, token + T, token)
        pick = jnp.where(token == lax.broadcasted_iota(jnp.int32, (T, T), 1), 1.0, 0.0).astype(BF16)
        placed = jnp.dot(pick, chunk_ref[...], preferred_element_type=F32)

        def body(i, carry):
            rows = pl.ds(pl.multiple_of(i * T, T), T)
            off = i * T + lax.broadcasted_iota(jnp.int32, (T, 1), 0) - shift
            off = jnp.where(off < 0, off + W, off)
            cache[rows, :] = jnp.where(off < T, placed, cache[rows, :].astype(F32)).astype(BF16)
            return carry

        lax.fori_loop(0, W // T, body, 0)
        copy = pltpu.make_async_copy(cache, out_hbm, loc_sem.at[sem])
        copy.start()
        return copy

    chips = (opp, right, left, chip)

    def scatter(part, prec, rel, fin, u, d_send, d_recv, r_send, r_recv):
        rows = part.shape[3] // 2

        def view(ref, d, half):
            return ref.at[core, d, u, pl.ds(half * rows, rows)]

        def to_partner(o):
            return pltpu.make_async_remote_copy(
                part.at[other, chips[o], u], prec.at[chips[o], u], d_send.at[u, o], d_recv.at[u, o],
                device_id={"tp": partner}, device_id_type=MESH)

        def ring(src, dst, k, dev):
            return pltpu.make_async_remote_copy(src, dst, r_send.at[u, k], r_recv.at[u, k], device_id={"tp": dev}, device_id_type=MESH)

        opp_a = ring(view(part, opp, 0), rel.at[0, u], 0, right_dev)
        opp_b = ring(view(part, opp, 1), rel.at[1, u], 1, left_dev)
        right_a = ring(view(part, right, 0), fin.at[0, u], 2, right_dev)
        right_b = ring(view(part, right, 1), fin.at[1, u], 3, right_dev)
        left_a = ring(view(part, left, 0), fin.at[2, u], 4, left_dev)
        left_b = ring(view(part, left, 1), fin.at[3, u], 5, left_dev)

        def add_partner(o):
            to_partner(o).wait_recv()
            d = chips[o]
            mine = part[core, d, u].astype(F32) + prec[d, u].astype(F32)
            part[core, d, u] = mine.astype(BF16)

        def first():
            add_partner(0)
            opp_a.start()
            opp_b.start()
            add_partner(1)
            right_b.start()
            add_partner(2)
            left_a.start()

        def relay():
            opp_a.wait_recv()
            a = view(part, right, 0)
            a[...] = (a[...].astype(F32) + rel[0, u].astype(F32)).astype(BF16)
            right_a.start()
            opp_b.wait_recv()
            b = view(part, left, 1)
            b[...] = (b[...].astype(F32) + rel[1, u].astype(F32)).astype(BF16)
            left_b.start()

        def total():
            to_partner(3).wait_recv()
            for c in (right_a, right_b, left_a, left_b):
                c.wait_recv()
            mine = part[core, chip, u].astype(F32) + prec[chip, u].astype(F32)
            out = []
            for half in range(2):
                sl = slice(half * rows, (half + 1) * rows)
                out.append(mine[sl] + fin[half, u].astype(F32) + fin[2 + half, u].astype(F32))
            return out

        def drain():
            for o in range(4):
                to_partner(o).wait_send()
            for c in (opp_a, opp_b, right_a, right_b, left_a, left_b):
                c.wait_send()

        return to_partner, first, relay, total, drain

    rs1 = [scatter(part1, prec1, rel1, fin1, u, d1_send, d1_recv, r1_send, r1_recv) for u in range(2)]
    def project_out(u):
        o_u = obuf[u]
        for o in range(4):
            d = chips[o]
            res = jnp.dot(o_u, wo[:, pl.ds(pl.multiple_of(d * dchip, dchip), dchip)], preferred_element_type=F32).astype(BF16)
            for c in range(2):
                part1[c, d, u] = res[:, c * dblk:(c + 1) * dblk]
            rs1[u][0](o).start()

    my_cols = pl.ds(pl.multiple_of(me * dblk, 128), dblk)
    a2_a, a2_b, a2_arrive, a2_drain = gather(g2, a2_send, a2_recv)

    def hidden_rows(u):
        per = half_n // TL
        hb = []
        for half, sums in enumerate(rs1[u][3]()):
            xs = jnp.concatenate([g1[u * per + half * (per // 2) + i, :, my_cols] for i in range(per // 2)], axis=0)
            hid = (xs.astype(F32) + sums).astype(BF16)
            g2[own, u * half_n + half * (half_n // 2):u * half_n + (half + 1) * (half_n // 2), :] = hid
            h32 = hid.astype(F32)
            hb.append(jnp.sum(h32 * h32, axis=-1, keepdims=True))
        return hb

    with scope("att00"):
        vc_copy.wait()
        attend(0, 0)
    with scope("att01"):
        attend(0, 1)
    with scope("out0"):
        wo_copy.wait()
        project_out(0)
    with scope("att10"):
        attend(1, 0)
    with scope("rs10_first"):
        rs1[0][1]()
    with scope("att11"):
        attend(1, 1)
    with scope("out1"):
        project_out(1)
    with scope("rs10_relay"):
        rs1[0][2]()
    with scope("rs11_first"):
        rs1[1][1]()
    with scope("rs10_total"):
        ss = hidden_rows(0)
        for c in a2_a:
            c.start()
    with scope("rs11_relay"):
        rs1[1][2]()
    with scope("rs11_total"):
        ss = ss + hidden_rows(1)
        ssbuf[own] = jnp.broadcast_to(jnp.concatenate(ss, axis=0), (T, T)).T[0:8]

    def ss_copy(src, k):
        dev = lax.rem(me + k, n_dev)
        return pltpu.make_async_remote_copy(ssbuf.at[src], ssbuf.at[src], ss_send.at[k - 1], ss_recv.at[k - 1], device_id={"tp": dev}, device_id_type=MESH)

    for k in range(1, n_dev):
        ss_copy(own, k).start()
    for c in a2_b:
        c.start()
    with scope("caches"):
        k_out = new_cache(kc, kch_ref, kn_hbm, 4)
        v_out = new_cache(vc, vch_ref, vn_hbm, 5)
    with scope("ss_wait"):
        for k in range(1, n_dev):
            ss_copy(lax.rem(me + n_dev - k, n_dev), k).wait_recv()
    tot = ssbuf[0]
    for k in range(1, n_dev):
        tot = tot + ssbuf[k]
    inv_row = lax.rsqrt(tot[0:1] * (1.0 / D) + NORM_EPS)
    inv = jnp.broadcast_to(inv_row, (T, T)).T[:, 0:1]

    def gate_up(s):
        d = order[s]
        for c in range(2):
            b = 2 * d + c
            gain = jnp.concatenate([mgain[pl.ds(b * (dblk // HD) + i, 1), :] for i in range(dblk // HD)], axis=1)
            mbuf[:, c * dblk:(c + 1) * dblk] = (g2[b].astype(F32) * inv * gain).astype(BF16)
        gu_wait(s)
        for n in range(gu_n):
            part = jnp.dot(mbuf[...], arena[gu_base(s) + n * dchip:gu_base(s) + (n + 1) * dchip, :], preferred_element_type=F32)
            if s:
                part = acc[:, n * SLOT:(n + 1) * SLOT] + part
            acc[:, n * SLOT:(n + 1) * SLOT] = part

    with scope("a2_0"):
        a2_arrive(PMA)
        a2_arrive(LA)
        a2_arrive(RB)
        a2_arrive(PMB)
    with scope("gu0"):
        gate_up(0)
        wd_half = wd_sem.shape[0] // 2
        for j in range(wd_half):
            wd_copy(j).start()
    with scope("a2_1"):
        for s in (RA, LB, PLA, PLB):
            a2_arrive(s)
    with scope("gu1"):
        gate_up(1)
        for j in range(wd_half, 2 * wd_half):
            wd_copy(j).start()
    with scope("a2_2"):
        a2_arrive(OA)
        a2_arrive(OB)
        a2_arrive(PRA)
        a2_arrive(PRB)
    with scope("gu2"):
        gate_up(2)
    with scope("a2_3"):
        a2_arrive(POA)
        a2_arrive(POB)
    with scope("gu3"):
        gate_up(3)
    with scope("silu"):
        for c0 in range(0, F, 256):
            gate = acc[:, c0:c0 + 256]
            up = acc[:, F + c0:F + c0 + 256]
            ubuf[:, c0:c0 + 256] = (gate * (1.0 / (1.0 + jnp.exp(-gate))) * up).astype(BF16)

    n_q = D // Q_COLS
    per_q = Q_COLS // SLOT
    rs2 = [scatter(part2, prec2, rel2, fin2, q, d2_send, d2_recv, r2_send, r2_recv) for q in range(n_q)]

    def down(q):
        for jj in range(per_q):
            j = q * per_q + jj
            wd_copy(j).wait()
            res = jnp.dot(ubuf[...], arena[wd_base + j * F:wd_base + (j + 1) * F, :], preferred_element_type=F32).astype(BF16)
            for b in range(n_dev):
                part2[b % 2, b // 2, q, :, jj * SLOT:(jj + 1) * SLOT] = res[b * TL:(b + 1) * TL]
        for o in range(4):
            rs2[q][0](o).start()

    def finish(q):
        sums = jnp.concatenate(rs2[q][3](), axis=0)
        tok = pl.ds(pl.multiple_of(me * TL, TL), TL)
        for k in range(Q_COLS // HD):
            at = q * Q_COLS + k * HD
            hid = g2[at // dblk, tok, at % dblk:at % dblk + HD]
            xout_ref[:, at:at + HD] = (hid.astype(F32) + sums[:, k * HD:(k + 1) * HD]).astype(BF16)

    for q in range(n_q + 2):
        if q < n_q:
            with scope(f"down{q}"):
                down(q)
        if 0 <= q - 1 < n_q:
            with scope(f"rs2{q - 1}_first"):
                rs2[q - 1][1]()
        if 0 <= q - 2 < n_q:
            with scope(f"rs2{q - 2}_relay"):
                rs2[q - 2][2]()
    for q in range(n_q):
        with scope(f"rs2{q}_total"):
            finish(q)

    a1_drain()
    a2_drain()
    for k in range(1, n_dev):
        ss_copy(own, k).wait_send()
    for r in rs1 + rs2:
        r[4]()
    k_out.wait()
    v_out.wait()


def solution(mesh):
    row_spec = P('dp', 'tp', None)
    cache_spec = P('dp', None, 'tp', None)
    head_cols = P(None, 'tp', None)
    in_specs = (row_spec, P('dp'), cache_spec, cache_spec, P(), head_cols, head_cols, head_cols, P('tp', None, None), P(), P(None, 'tp'), P(None, 'tp'), P('tp', None))
    out_specs = (row_spec, cache_spec, cache_spec)
    n_dev = mesh.shape['tp']

    def local_layer(x_in, start_pos, k_cache, v_cache, attn_gain, w_query, w_key, w_value, w_out, mlp_gain, w_gate, w_up, w_down):
        _, TL, D = x_in.shape
        W, HD = k_cache.shape[1], k_cache.shape[3]
        G = w_query.shape[1]
        F = w_gate.shape[1]
        T = TL * n_dev
        n_chip = n_dev // 2
        dblk, dchip = D // n_dev, D // n_chip
        inv_freq = np.repeat(np.power(ROPE_BASE, -np.arange(0, HD, 2) / HD), 2).astype(np.float32)
        vmem = pl.BlockSpec(memory_space=pltpu.VMEM)
        hbm = pl.BlockSpec(memory_space=pl.ANY)
        smem = pl.BlockSpec(memory_space=pltpu.SMEM)
        gu_n = 2 * F // SLOT
        V = pltpu.VMEM
        dma = pltpu.SemaphoreType.DMA
        half = T // 2
        n_q = D // Q_COLS
        scratch = [
            V((n_dev, TL, D), BF16), V((n_dev, T, dblk), BF16), V((T, D), BF16), V((T, dchip), BF16),
            V((2, n_chip, 2, half, dblk), BF16), V((2, n_chip, n_q, TL, Q_COLS), BF16),
            V((n_chip, 2, half, dblk), BF16), V((n_chip, n_q, TL, Q_COLS), BF16),
            V((2, 2, half // 2, dblk), BF16), V((2, n_q, TL // 2, Q_COLS), BF16),
            V((4, 2, half // 2, dblk), BF16), V((4, n_q, TL // 2, Q_COLS), BF16),
            V((n_dev, 8, T), F32),
            V((n_chip * gu_n * dchip, SLOT), BF16), V((G * HD, D), BF16), V((512, HD), F32),
            V((HD, W), BF16), V((W, HD), BF16), V((W, HD), BF16),
            V((2, G * half, HD), BF16), V((2 * half, W), F32), V((2, half, G * HD), BF16),
            V((T, 2 * F), F32), V((T, F), BF16), V((T, HD), BF16), V((T, HD), BF16), V((D // HD, HD), F32), V((D // HD, HD), F32), V((T, HD), F32), V((T, HD), F32),
            dma((6,)), dma((SLOT // HD,)), dma((4,)), dma((n_chip,)), dma((D // SLOT,)),
            dma((14,)), dma((14,)), dma((14,)), dma((14,)), dma((n_dev - 1,)), dma((n_dev - 1,)),
            dma((2, 4)), dma((2, 4)), dma((n_q, 4)), dma((n_q, 4)),
            dma((2, 6)), dma((2, 6)), dma((n_q, 6)), dma((n_q, 6)),
        ]
        x_out, k_new, v_new = pl.pallas_call(
            functools.partial(layer_kernel, n_dev, (D, T, TL, HD, F, W, G)),
            out_shape=[jax.ShapeDtypeStruct((TL, D), BF16), jax.ShapeDtypeStruct((W, HD), BF16), jax.ShapeDtypeStruct((W, HD), BF16)],
            in_specs=[smem, hbm, hbm, hbm, vmem, hbm, hbm, hbm, hbm, vmem, hbm, hbm, hbm, vmem],
            out_specs=[vmem, hbm, hbm],
            scratch_shapes=scratch,
            compiler_params=pltpu.CompilerParams(collective_id=0, has_side_effects=True, vmem_limit_bytes=67043328),
            name="layer",
        )(
            start_pos, x_in[0], k_cache.reshape(W, HD), v_cache.reshape(W, HD), attn_gain.reshape(D // HD, HD),
            w_query.reshape(D * G, HD), w_key.reshape(D, HD), w_value.reshape(D, HD), w_out.reshape(G * HD, D),
            mlp_gain.reshape(D // HD, HD), w_gate, w_up, w_down, inv_freq[None, :],
        )
        return x_out[None], k_new.reshape(k_cache.shape), v_new.reshape(v_cache.shape)

    return jax.shard_map(local_layer, mesh=mesh, in_specs=in_specs, out_specs=out_specs, check_vma=False)
```

time: 97.9 us -> 73.2 us (0.75)
  Pallas kernels: 82.5 us -> 65.5 us
  other arithmetic: 10 us -> 0 us
  local copies, waits for them, and re-layouts: 3.65 us -> 6.12 us
    pallas_call x1, Pallas kernels: 82.5 us -> 65.5 us  [local_layer(): pl.pallas_call(functools.partial(layer_kernel, n_dev, (D, T, TL, HD, F, W...]
    select_n x2 -> x0, other arithmetic: 8.43 us -> none  [the longest x1 8.43 us: one_row(): return jnp.where((offsets < chunk_len)[:, None, None], placed, old_rows)]
    unnamed x3, local copies, waits for them, and re-layouts: 0.67 us -> 6.12 us
    reshape x2 -> x0, local copies, waits for them, and re-layouts: 2.63 us -> none  [the longest x1 1.32 us: local_layer(): attn_gain.reshape(1, D)]
where the time goes in v2:
time: 73.2 us; the launch traced here: 72.9 us
  Pallas kernels  65.5 us (89%)
  local copies, waits for them, and re-layouts  6.12 us (8%)
  between operations  1.29 us (2%)
    pallas_call x1, Pallas kernels, local_layer(): pl.pallas_call(functools.partial(layer_kernel, n_dev, (D, T, TL, HD, F, W...  65.5 us
    unnamed x3, local copies, waits for them, and re-layouts  6.12 us

profile of v2, /device:TPU:112, one launch (start us, length us, event | category | flops | bytes accessed | tf_op | source)
XLA Modules:
  0.0 72.9 jit_solution(15128834092854281048)
XLA Ops:
  1.3 65.5 %layer.1 = (bf16[16,5120]{1,0:T(8,128)(2,1)}, bf16[4096,128]{1,0:T(8,128)(2,1)}, bf16[4096,128]{1,0:T(8,128)(2,1)}) custom-call(s32[1]{0:T(128)S(6)} %copy.20.start_ref, bf16[16,5120]{1,0:T(8,128)(2,1)} %bitcast.20, bf16[4096,128]{1,0:T(8,128)(2,1)} %bitcast.16, bf16[4096,128]{1,0:T(8,128)(2,1)} %bitcast.17, bf16[40,128]{1,0:T(8,128)(2,1)} %bitcast.22, ...), custom_call_target="tpu_custom_call" | custom-call | tf_op jit(solution)/shard_map/layer/pallas_call | solution.py:592
  66.8 1.6 %copy.21 = bf16[1,16,5120]{2,1,0:T(8,128)(2,1)} copy(bf16[1,16,5120]{2,1,0:T(8,128)(2,1)} %bitcast.21) | data formatting | bytes 327680
  68.4 2.3 %copy.22 = bf16[1,4096,1,128]{3,1,2,0:T(8,128)(2,1)} copy(bf16[1,4096,1,128]{3,1,2,0:T(8,128)(2,1)} %bitcast.19) | data formatting | bytes 2097152
  70.7 2.3 %copy.23 = bf16[1,4096,1,128]{3,1,2,0:T(8,128)(2,1)} copy(bf16[1,4096,1,128]{3,1,2,0:T(8,128)(2,1)} %bitcast.18) | data formatting | bytes 2097152
